TPU v7x, 32 devices: a whole 2x2x4 slice. The times are simulated.
32 devices in a mesh: section: 2 (over x), sht: 16 (over z, y, core).
Axes of the slice: x: 2, y: 2, z: 4, core: 2. Of those that a mesh axis runs over, the one named last changes fastest.
Arguments:
- analysis: bfloat16 [128, 256, 192], P('sht', None, 'section'), may hold values from -6 to 6
- perturbations: bfloat16 [6, 128, 256, 192], P(None, 'sht', None, 'section'), may hold values from -6 to 6
- gain_first: float32 [2, 192], P('section'), may hold values from 0.1 to 1.9
- spectral_gain: float32 [2, 2, 24576], P('section'), may hold values from -6 to 6
- skip_weight: bfloat16 [2, 192, 192], P('section'), may hold values from -0.4375 to 0.4375
- gain_second: float32 [2, 192], P('section'), may hold values from 0.1 to 1.9
- mlp_in: bfloat16 [2, 192, 384], P('section'), may hold values from -0.4375 to 0.4375
- mlp_out: bfloat16 [2, 192, 384], P('section'), may hold values from -0.3125 to 0.3125
Outputs:
- block_outputs: bfloat16 [2, 6, 128, 49152], P('section', None, 'sht')
All inputs are finite; a program needn't handle non-finite values.
Results may differ from a plain program's by a relative error of at most 0.025.
Values may be sent and summed in bfloat16 or wider, within the bound.
A program may use at most 64 MiB of HBM per device.

v0:
```python
import math
import jax
import jax.numpy as jnp
from jax import lax
from jax.sharding import PartitionSpec as P

C = 192
NLAT = 128
NLON = 256
LMAX = 128
MMAX = 128


def shifted_2(value, axis, steps):
    count = lax.axis_size(axis)
    first, last = (max(0, -steps), min(count, count - steps))
    return lax.ppermute(value, axis, [(source, source + steps) for source in range(first, last)])


def legendre_table(nlat, lmax, mmax, nlon, m_first, m_count):
    latitudes = jnp.arange(nlat, dtype=jnp.float32)
    colatitude = math.pi * (latitudes + 0.5) / nlat
    cosine = jnp.cos(colatitude)
    sine = jnp.sin(colatitude)
    orders = jnp.arange(1, mmax, dtype=jnp.float32)
    factors = jnp.cumsum(0.5 * jnp.log((2.0 * orders + 1.0) / (2.0 * orders)))
    log_diag = jnp.concatenate([jnp.zeros((1,), jnp.float32), factors])
    m_index = m_first + jnp.arange(m_count, dtype=jnp.int32)
    picked = jnp.sum(
        jnp.where(
            m_index[:, None] == jnp.arange(mmax, dtype=jnp.int32)[None, :], log_diag[None, :], 0.0
        ),
        axis=1,
    )
    m_float = m_index.astype(jnp.float32)
    diagonal = jnp.exp(picked[None, :] + m_float[None, :] * jnp.log(sine)[:, None]) * math.sqrt(
        0.25 / math.pi
    )
    cos_col = cosine[:, None]

    def advance(carry, degree):
        latest, earlier = carry
        degree_float = degree.astype(jnp.float32)
        lower = jnp.sqrt(
            (4.0 * degree_float * degree_float - 1.0)
            / jnp.maximum(degree_float * degree_float - m_float * m_float, 1.0)
        )
        shifted = degree_float - 1.0
        upper = jnp.sqrt(
            jnp.maximum(shifted * shifted - m_float * m_float, 0.0)
            / jnp.maximum(4.0 * shifted * shifted - 1.0, 1.0)
        )
        recurred = lower[None, :] * (cos_col * latest - upper[None, :] * earlier)
        first_step = jnp.sqrt(2.0 * m_float + 3.0)[None, :] * cos_col * diagonal
        current = jnp.where(
            degree == m_index[None, :],
            diagonal,
            jnp.where(
                degree == m_index[None, :] + 1,
                first_step,
                jnp.where(degree > m_index[None, :] + 1, recurred, 0.0),
            ),
        )
        return ((current, latest), current)

    initial = jnp.zeros((nlat, m_count), jnp.float32)
    _, stacked = lax.scan(advance, (initial, initial), jnp.arange(lmax, dtype=jnp.int32), unroll=8)
    legendre = jnp.transpose(stacked, (1, 0, 2))
    weights = sine * (2.0 * math.pi / nlon) * (math.pi / nlat)
    return (legendre, weights)


def fourier_tables(nlon, mmax):
    samples = jnp.arange(nlon, dtype=jnp.int32)
    orders = jnp.arange(mmax, dtype=jnp.int32)
    phase = (samples[:, None] * orders[None, :] % nlon).astype(jnp.float32) * (2.0 * math.pi / nlon)
    cosines = jnp.cos(phase)
    sines = jnp.sin(phase)
    forward = jnp.stack([cosines, -sines], axis=1).astype(jnp.bfloat16)
    factor = jnp.where(orders == 0, 1.0, 2.0).astype(jnp.float32)
    inverse = jnp.stack([cosines.T * factor[:, None], -sines.T * factor[:, None]], axis=0).astype(
        jnp.bfloat16
    )
    return (forward, inverse)


def layer_norm(values, gain_vector):
    average = jnp.mean(values, axis=-1, keepdims=True)
    centred = values - average
    variance = jnp.mean(centred * centred, axis=-1, keepdims=True)
    return centred * lax.rsqrt(variance + 1e-05) * gain_vector


def apply_gain(coeffs, gain_table):
    real_part = coeffs[:, :, :, 0]
    imag_part = coeffs[:, :, :, 1]
    gain_real = gain_table[0][None, :, None, :]
    gain_imag = gain_table[1][None, :, None, :]
    return jnp.stack(
        [
            real_part * gain_real - imag_part * gain_imag,
            real_part * gain_imag + imag_part * gain_real,
        ],
        axis=3,
    )


def recenter(analysis, perturbations):
    pert_wide = perturbations.astype(jnp.float32)
    average = jnp.mean(pert_wide, axis=0, keepdims=True)
    return (analysis.astype(jnp.float32)[None] + pert_wide - average).astype(jnp.bfloat16)


def project_out(hidden, out_matrix):
    return lax.dot_general(
        hidden, out_matrix, (((1,), (1,)), ((), ())), preferred_element_type=jnp.float32
    )


def per_device(
    analysis, perturbations, gain_first, spectral_gain, skip_weight, gain_second, mlp_in, mlp_out
):
    section_index = lax.axis_index("section")
    section_count = lax.axis_size("section")
    member_count = perturbations.shape[0]
    stacked = jnp.concatenate([analysis[None], perturbations], axis=0)
    gathered = lax.all_gather(stacked, "section", axis=3, tiled=True)
    members = recenter(gathered[0], gathered[1:])
    forward, inverse = fourier_tables(NLON, MMAX)
    full_gain = spectral_gain[0].reshape(2, LMAX, C)
    m_count = MMAX // lax.axis_size("sht")
    legendre, weights = legendre_table(
        NLAT, LMAX, MMAX, NLON, lax.axis_index("sht") * m_count, m_count
    )
    weighted = (legendre * weights[:, None, None]).astype(jnp.bfloat16)
    plain_table = legendre.astype(jnp.bfloat16)

    def spectral(normed):
        batch_rows = normed.shape[0]
        lat_rows = normed.shape[1]
        spectrum = jnp.einsum(
            "bjkc,kpm->bjmpc", normed, forward, preferred_element_type=jnp.float32
        ).astype(jnp.bfloat16)
        spectrum = spectrum.reshape(batch_rows, lat_rows, MMAX, 2 * C)
        exchanged = lax.all_to_all(spectrum, "sht", split_axis=2, concat_axis=1, tiled=True)
        item_count = exchanged.shape[0]
        coeffs = jnp.einsum(
            "jlm,bjmq->blmq", weighted, exchanged, preferred_element_type=jnp.float32
        )
        coeffs = coeffs.reshape(item_count, LMAX, m_count, 2, C)
        filtered = (
            apply_gain(coeffs, full_gain)
            .astype(jnp.bfloat16)
            .reshape(item_count, LMAX, m_count, 2 * C)
        )
        returned = jnp.einsum(
            "jlm,blmq->bjmq", plain_table, filtered, preferred_element_type=jnp.float32
        ).astype(jnp.bfloat16)
        returned = lax.all_to_all(returned, "sht", split_axis=1, concat_axis=2, tiled=True)
        returned = returned.reshape(batch_rows, lat_rows, MMAX, 2, C)
        return jnp.einsum("bjmpc,pmk->bjkc", returned, inverse, preferred_element_type=jnp.float32)

    def sfno_block(current_state):
        state_wide = current_state.astype(jnp.float32)
        channels = current_state.shape[-1]
        normed = layer_norm(state_wide, gain_first[0]).astype(jnp.bfloat16)
        spatial = spectral(normed)
        skipped = jnp.dot(
            normed.reshape(-1, channels), skip_weight[0], preferred_element_type=jnp.float32
        ).reshape(spatial.shape)
        activated = jax.nn.gelu(spatial + skipped, approximate=False)
        second = layer_norm(activated, gain_second[0]).astype(jnp.bfloat16)
        hidden = jax.nn.gelu(
            jnp.dot(second.reshape(-1, channels), mlp_in[0], preferred_element_type=jnp.float32),
            approximate=False,
        ).astype(jnp.bfloat16)
        update = project_out(hidden, mlp_out[0]).reshape(spatial.shape)
        return (state_wide + update).astype(jnp.bfloat16)

    batch_size = 1
    batch_count = member_count // batch_size
    tick_count = section_count + batch_count - 1

    def tick(tick_index, carry):
        current_state, stored = carry
        received = shifted_2(current_state, "section", 1)
        first_rows = lax.dynamic_slice_in_dim(
            members, jnp.minimum(tick_index, batch_count - 1) * batch_size, batch_size, 0
        )
        incoming = jnp.where(section_index == 0, first_rows, received)
        result = sfno_block(incoming)
        position = tick_index - section_index
        is_valid = jnp.logical_and(position >= 0, position < batch_count)
        offset = jnp.clip(position, 0, batch_count - 1) * batch_size
        previous = lax.dynamic_slice_in_dim(stored, offset, batch_size, 0)
        stored = lax.dynamic_update_slice_in_dim(
            stored, jnp.where(is_valid, result, previous), offset, 0
        )
        return (result, stored)

    empty_state = jnp.zeros((batch_size,) + members.shape[1:], jnp.bfloat16)
    _, stored = lax.fori_loop(0, tick_count, tick, (empty_state, jnp.zeros_like(members)))
    merged = stored.reshape(stored.shape[0], stored.shape[1], stored.shape[2] * stored.shape[3])
    return merged[None]


def solution(mesh):
    return jax.shard_map(
        per_device,
        mesh=mesh,
        in_specs=(
            P("sht", None, "section"),
            P(None, "sht", None, "section"),
            P("section", None),
            P("section", None, None),
            P("section", None, None),
            P("section", None),
            P("section", None, None),
            P("section", None, None),
        ),
        out_specs=P("section", None, "sht", None),
        check_vma=False,
    )
```

profile of v0, /device:TPU:11, one launch (start us, length us, event | category | flops | bytes accessed | tf_op | source)
XLA Modules:
  0.0 980.3 jit_solution(16120760669115899107)
XLA Ops:
  10.8 264.0 %while.39 = (s32[]{:T(128)}, f32[128,8]{0,1:T(8,128)S(1)}, f32[128,8]{0,1:T(8,128)S(1)}, f32[16,8,128,8]{2,3,1,0:T(8,128)S(1)}, s32[16,8]{0,1:T(8,128)S(1)}, /*i...) while((s32[]{:T(128)}, f32[128,8]{0,1:T(8,128)S(1)}, ...), condition=%wide.region_4.5_spmd.clone.clone.clone.clone, body=%wide.region_3.4_spmd.clone.clone.clone.clone.sunk | while | flops 102682 | bytes 236492 | solution.py:67
  288.7 666.6 %while.38 = (s32[]{:T(128)}, bf16[1,8,256,192]{2,3,1,0:T(8,128)(2,1)S(1)}, bf16[6,8,256,192]{2,3,1,0:T(8,128)(2,1)}, pred[]{:T(512)}, bf16[6,8,256,192]{2,3,1,0:...) while((s32[]{:T(128)}, ...), condition=%wide.region_10.11_spmd.clone, body=%wide.region_5.10_spmd.clone.sunk | while | flops 1450184704 | bytes 59488172 | solution.py:202
  290.0 19.0 %collective-permute-done = bf16[1,8,256,192]{2,3,1,0:T(8,128)(2,1)S(1)} collective-permute-done((bf16[1,8,256,192]{2,3,1,0:T(8,128)(2,1)S(1)}, bf16[1,8,256,192]{2,3,1,0:T(8,128)(2,1)S(1)}, u32[]{:S(2)}, u32[]{:S(2)}) %collective-permute-start) | collective-permute-done | bytes 786464 | tf_op jit(solution)/shard_map/while/body/eval_jaxpr/ppermute | solution.py:17
  320.9 19.6 %all-to-all-done = bf16[1,8,128,384]{3,1,0,2:T(8,128)(2,1)S(1)} async-done(((bf16[1,8,128,384]{3,1,0,2:T(8,128)(2,1)}), bf16[1,8,128,384]{3,1,0,2:T(8,128)(2,1)S(1)}, u32[]{:S(2)}, u32[]{:S(2)}) %all-to-all-start) | async-done | bytes 786464 | tf_op jit(solution)/shard_map/while/body/eval_jaxpr/all_to_all | solution.py:145
  347.6 19.6 %all-to-all-done.1 = bf16[1,128,8,384]{3,2,0,1:T(8,128)(2,1)S(1)} async-done(((bf16[1,128,8,384]{3,2,0,1:T(8,128)(2,1)}), bf16[1,128,8,384]{3,2,0,1:T(8,128)(2,1)S(1)}, u32[]{:S(2)}, u32[]{:S(2)}) %all-to-all-start.1) | async-done | bytes 786464 | tf_op jit(solution)/shard_map/while/body/eval_jaxpr/all_to_all | solution.py:159
  374.8 7.5 fusion.153
  386.6 20.1 %collective-permute-done = bf16[1,8,256,192]{2,3,1,0:T(8,128)(2,1)S(1)} collective-permute-done((bf16[1,8,256,192]{2,3,1,0:T(8,128)(2,1)S(1)}, bf16[1,8,256,192]{2,3,1,0:T(8,128)(2,1)S(1)}, u32[]{:S(2)}, u32[]{:S(2)}) %collective-permute-start) | collective-permute-done | bytes 786464 | tf_op jit(solution)/shard_map/while/body/eval_jaxpr/ppermute | solution.py:17
  415.9 19.6 %all-to-all-done = bf16[1,8,128,384]{3,1,0,2:T(8,128)(2,1)S(1)} async-done(((bf16[1,8,128,384]{3,1,0,2:T(8,128)(2,1)}), bf16[1,8,128,384]{3,1,0,2:T(8,128)(2,1)S(1)}, u32[]{:S(2)}, u32[]{:S(2)}) %all-to-all-start) | async-done | bytes 786464 | tf_op jit(solution)/shard_map/while/body/eval_jaxpr/all_to_all | solution.py:145
  442.6 19.6 %all-to-all-done.1 = bf16[1,128,8,384]{3,2,0,1:T(8,128)(2,1)S(1)} async-done(((bf16[1,128,8,384]{3,2,0,1:T(8,128)(2,1)}), bf16[1,128,8,384]{3,2,0,1:T(8,128)(2,1)S(1)}, u32[]{:S(2)}, u32[]{:S(2)}) %all-to-all-start.1) | async-done | bytes 786464 | tf_op jit(solution)/shard_map/while/body/eval_jaxpr/all_to_all | solution.py:159
  469.8 7.5 fusion.153
  481.6 20.1 %collective-permute-done = bf16[1,8,256,192]{2,3,1,0:T(8,128)(2,1)S(1)} collective-permute-done((bf16[1,8,256,192]{2,3,1,0:T(8,128)(2,1)S(1)}, bf16[1,8,256,192]{2,3,1,0:T(8,128)(2,1)S(1)}, u32[]{:S(2)}, u32[]{:S(2)}) %collective-permute-start) | collective-permute-done | bytes 786464 | tf_op jit(solution)/shard_map/while/body/eval_jaxpr/ppermute | solution.py:17
  510.9 19.6 %all-to-all-done = bf16[1,8,128,384]{3,1,0,2:T(8,128)(2,1)S(1)} async-done(((bf16[1,8,128,384]{3,1,0,2:T(8,128)(2,1)}), bf16[1,8,128,384]{3,1,0,2:T(8,128)(2,1)S(1)}, u32[]{:S(2)}, u32[]{:S(2)}) %all-to-all-start) | async-done | bytes 786464 | tf_op jit(solution)/shard_map/while/body/eval_jaxpr/all_to_all | solution.py:145
  537.7 19.6 %all-to-all-done.1 = bf16[1,128,8,384]{3,2,0,1:T(8,128)(2,1)S(1)} async-done(((bf16[1,128,8,384]{3,2,0,1:T(8,128)(2,1)}), bf16[1,128,8,384]{3,2,0,1:T(8,128)(2,1)S(1)}, u32[]{:S(2)}, u32[]{:S(2)}) %all-to-all-start.1) | async-done | bytes 786464 | tf_op jit(solution)/shard_map/while/body/eval_jaxpr/all_to_all | solution.py:159
  564.8 7.5 fusion.153
  576.6 20.1 %collective-permute-done = bf16[1,8,256,192]{2,3,1,0:T(8,128)(2,1)S(1)} collective-permute-done((bf16[1,8,256,192]{2,3,1,0:T(8,128)(2,1)S(1)}, bf16[1,8,256,192]{2,3,1,0:T(8,128)(2,1)S(1)}, u32[]{:S(2)}, u32[]{:S(2)}) %collective-permute-start) | collective-permute-done | bytes 786464 | tf_op jit(solution)/shard_map/while/body/eval_jaxpr/ppermute | solution.py:17
  605.9 19.6 %all-to-all-done = bf16[1,8,128,384]{3,1,0,2:T(8,128)(2,1)S(1)} async-done(((bf16[1,8,128,384]{3,1,0,2:T(8,128)(2,1)}), bf16[1,8,128,384]{3,1,0,2:T(8,128)(2,1)S(1)}, u32[]{:S(2)}, u32[]{:S(2)}) %all-to-all-start) | async-done | bytes 786464 | tf_op jit(solution)/shard_map/while/body/eval_jaxpr/all_to_all | solution.py:145
  632.7 19.6 %all-to-all-done.1 = bf16[1,128,8,384]{3,2,0,1:T(8,128)(2,1)S(1)} async-done(((bf16[1,128,8,384]{3,2,0,1:T(8,128)(2,1)}), bf16[1,128,8,384]{3,2,0,1:T(8,128)(2,1)S(1)}, u32[]{:S(2)}, u32[]{:S(2)}) %all-to-all-start.1) | async-done | bytes 786464 | tf_op jit(solution)/shard_map/while/body/eval_jaxpr/all_to_all | solution.py:159
  659.8 7.5 fusion.153
  671.6 20.1 %collective-permute-done = bf16[1,8,256,192]{2,3,1,0:T(8,128)(2,1)S(1)} collective-permute-done((bf16[1,8,256,192]{2,3,1,0:T(8,128)(2,1)S(1)}, bf16[1,8,256,192]{2,3,1,0:T(8,128)(2,1)S(1)}, u32[]{:S(2)}, u32[]{:S(2)}) %collective-permute-start) | collective-permute-done | bytes 786464 | tf_op jit(solution)/shard_map/while/body/eval_jaxpr/ppermute | solution.py:17
  700.9 19.6 %all-to-all-done = bf16[1,8,128,384]{3,1,0,2:T(8,128)(2,1)S(1)} async-done(((bf16[1,8,128,384]{3,1,0,2:T(8,128)(2,1)}), bf16[1,8,128,384]{3,1,0,2:T(8,128)(2,1)S(1)}, u32[]{:S(2)}, u32[]{:S(2)}) %all-to-all-start) | async-done | bytes 786464 | tf_op jit(solution)/shard_map/while/body/eval_jaxpr/all_to_all | solution.py:145
  727.7 19.6 %all-to-all-done.1 = bf16[1,128,8,384]{3,2,0,1:T(8,128)(2,1)S(1)} async-done(((bf16[1,128,8,384]{3,2,0,1:T(8,128)(2,1)}), bf16[1,128,8,384]{3,2,0,1:T(8,128)(2,1)S(1)}, u32[]{:S(2)}, u32[]{:S(2)}) %all-to-all-start.1) | async-done | bytes 786464 | tf_op jit(solution)/shard_map/while/body/eval_jaxpr/all_to_all | solution.py:159
  754.8 7.5 fusion.153
  766.7 20.1 %collective-permute-done = bf16[1,8,256,192]{2,3,1,0:T(8,128)(2,1)S(1)} collective-permute-done((bf16[1,8,256,192]{2,3,1,0:T(8,128)(2,1)S(1)}, bf16[1,8,256,192]{2,3,1,0:T(8,128)(2,1)S(1)}, u32[]{:S(2)}, u32[]{:S(2)}) %collective-permute-start) | collective-permute-done | bytes 786464 | tf_op jit(solution)/shard_map/while/body/eval_jaxpr/ppermute | solution.py:17
  795.9 19.6 %all-to-all-done = bf16[1,8,128,384]{3,1,0,2:T(8,128)(2,1)S(1)} async-done(((bf16[1,8,128,384]{3,1,0,2:T(8,128)(2,1)}), bf16[1,8,128,384]{3,1,0,2:T(8,128)(2,1)S(1)}, u32[]{:S(2)}, u32[]{:S(2)}) %all-to-all-start) | async-done | bytes 786464 | tf_op jit(solution)/shard_map/while/body/eval_jaxpr/all_to_all | solution.py:145
  822.7 19.6 %all-to-all-done.1 = bf16[1,128,8,384]{3,2,0,1:T(8,128)(2,1)S(1)} async-done(((bf16[1,128,8,384]{3,2,0,1:T(8,128)(2,1)}), bf16[1,128,8,384]{3,2,0,1:T(8,128)(2,1)S(1)}, u32[]{:S(2)}, u32[]{:S(2)}) %all-to-all-start.1) | async-done | bytes 786464 | tf_op jit(solution)/shard_map/while/body/eval_jaxpr/all_to_all | solution.py:159
  849.8 7.5 fusion.153
  861.7 20.1 %collective-permute-done = bf16[1,8,256,192]{2,3,1,0:T(8,128)(2,1)S(1)} collective-permute-done((bf16[1,8,256,192]{2,3,1,0:T(8,128)(2,1)S(1)}, bf16[1,8,256,192]{2,3,1,0:T(8,128)(2,1)S(1)}, u32[]{:S(2)}, u32[]{:S(2)}) %collective-permute-start) | collective-permute-done | bytes 786464 | tf_op jit(solution)/shard_map/while/body/eval_jaxpr/ppermute | solution.py:17
  890.9 19.6 %all-to-all-done = bf16[1,8,128,384]{3,1,0,2:T(8,128)(2,1)S(1)} async-done(((bf16[1,8,128,384]{3,1,0,2:T(8,128)(2,1)}), bf16[1,8,128,384]{3,1,0,2:T(8,128)(2,1)S(1)}, u32[]{:S(2)}, u32[]{:S(2)}) %all-to-all-start) | async-done | bytes 786464 | tf_op jit(solution)/shard_map/while/body/eval_jaxpr/all_to_all | solution.py:145
  917.7 19.6 %all-to-all-done.1 = bf16[1,128,8,384]{3,2,0,1:T(8,128)(2,1)S(1)} async-done(((bf16[1,128,8,384]{3,2,0,1:T(8,128)(2,1)}), bf16[1,128,8,384]{3,2,0,1:T(8,128)(2,1)S(1)}, u32[]{:S(2)}, u32[]{:S(2)}) %all-to-all-start.1) | async-done | bytes 786464 | tf_op jit(solution)/shard_map/while/body/eval_jaxpr/all_to_all | solution.py:159
  944.8 7.5 fusion.153
  955.3 8.0 copy.52
  963.2 10.2 %broadcast_in_dim_reshape.3 = bf16[1,6,8,49152]{3,2,1,0:T(8,128)(2,1)} reshape(bf16[6,8,256,192]{3,2,1,0:T(8,128)(2,1)} %copy.52) | data formatting | bytes 9437184 | tf_op jit(solution)/shard_map/broadcast_in_dim;reshape | solution.py:204
  (902 shorter events, 398.2 us)
Async XLA Ops:
  6.5 271.6 %all-gather.2.cloned.1.call-start = ((), (), s32[]{:S(2)}) async-start(), calls=%async_computation.2 | async-start | bytes 8257536 | tf_op jit(solution)/shard_map/all_gather | solution.py:127
  10.7 264.1 %copy-start.9 = (bf16[1,192,192]{2,1,0:T(8,128)(2,1)S(1)}, bf16[1,192,192]{2,1,0:T(8,128)(2,1)}, u32[]{:S(2)}) copy-start(bf16[1,192,192]{2,1,0:T(8,128)(2,1)} %param.16) | copy-start | bytes 221188
  10.8 264.8 %copy-start.8 = (f32[1,2,24576]{2,1,0:T(2,128)S(1)}, f32[1,2,24576]{2,1,0:T(2,128)}, u32[]{:S(2)}) copy-start(f32[1,2,24576]{2,1,0:T(2,128)} %param.15) | copy-start | bytes 589828
  288.7 52.0 %copy-start.3 = (bf16[128,128,8]{1,0,2:T(8,128)(2,1)}, bf16[128,128,8]{1,0,2:T(8,128)(2,1)S(1)}, u32[]{:S(2)}) copy-start(bf16[128,128,8]{1,0,2:T(8,128)(2,1)S(1)} %get-tuple-element.1292) | copy-start | bytes 786436 | tf_op jit(solution)/shard_map/while
  288.7 52.8 %copy-start.1 = (bf16[128,128,8]{1,0,2:T(8,128)(2,1)}, bf16[128,128,8]{1,0,2:T(8,128)(2,1)S(1)}, u32[]{:S(2)}) copy-start(bf16[128,128,8]{1,0,2:T(8,128)(2,1)S(1)} %get-tuple-element.1294) | copy-start | bytes 786436 | tf_op jit(solution)/shard_map/while
  288.7 20.3 %collective-permute-start = (bf16[1,8,256,192]{2,3,1,0:T(8,128)(2,1)S(1)}, bf16[1,8,256,192]{2,3,1,0:T(8,128)(2,1)S(1)}, u32[]{:S(2)}, u32[]{:S(2)}) collective-permute-start(bf16[1,8,256,192]{2,3,1,0:T(8,128)(2,1)S(1)} %broadcast_select_fusion.2), channel_id=1, source_target_pairs={{0,16},{1,17},{2,18},{3,19},{4,20},{5,21},{6,22},{7,23},{8,24},{9,... | collective-permute-start | bytes 2359304 | tf_op jit(solution)/shard_map/while/body/eval_jaxpr/ppermute | solution.py:17
  313.4 27.0 %all-to-all-start = ((bf16[1,8,128,384]{3,1,0,2:T(8,128)(2,1)}), bf16[1,8,128,384]{3,1,0,2:T(8,128)(2,1)S(1)}, u32[]{:S(2)}, u32[]{:S(2)}) async-start(bf16[1,8,128,384]{3,1,0,2:T(8,128)(2,1)} %copy.73), calls=%async_computation | async-start | bytes 1572864 | tf_op jit(solution)/shard_map/while/body/eval_jaxpr/all_to_all | solution.py:145
  343.2 24.1 %all-to-all-start.1 = ((bf16[1,128,8,384]{3,2,0,1:T(8,128)(2,1)}), bf16[1,128,8,384]{3,2,0,1:T(8,128)(2,1)S(1)}, u32[]{:S(2)}, u32[]{:S(2)}) async-start(bf16[1,128,8,384]{3,2,0,1:T(8,128)(2,1)} %copy.76), calls=%async_computation.1 | async-start | bytes 1572864 | tf_op jit(solution)/shard_map/while/body/eval_jaxpr/all_to_all | solution.py:159
  385.2 51.2 %copy-start.1 = (bf16[128,128,8]{1,0,2:T(8,128)(2,1)}, bf16[128,128,8]{1,0,2:T(8,128)(2,1)S(1)}, u32[]{:S(2)}) copy-start(bf16[128,128,8]{1,0,2:T(8,128)(2,1)S(1)} %get-tuple-element.1294) | copy-start | bytes 786436 | tf_op jit(solution)/shard_map/while
  385.3 21.4 %collective-permute-start = (bf16[1,8,256,192]{2,3,1,0:T(8,128)(2,1)S(1)}, bf16[1,8,256,192]{2,3,1,0:T(8,128)(2,1)S(1)}, u32[]{:S(2)}, u32[]{:S(2)}) collective-permute-start(bf16[1,8,256,192]{2,3,1,0:T(8,128)(2,1)S(1)} %broadcast_select_fusion.2), channel_id=1, source_target_pairs={{0,16},{1,17},{2,18},{3,19},{4,20},{5,21},{6,22},{7,23},{8,24},{9,... | collective-permute-start | bytes 2359304 | tf_op jit(solution)/shard_map/while/body/eval_jaxpr/ppermute | solution.py:17
  411.1 24.4 %all-to-all-start = ((bf16[1,8,128,384]{3,1,0,2:T(8,128)(2,1)}), bf16[1,8,128,384]{3,1,0,2:T(8,128)(2,1)S(1)}, u32[]{:S(2)}, u32[]{:S(2)}) async-start(bf16[1,8,128,384]{3,1,0,2:T(8,128)(2,1)} %copy.73), calls=%async_computation | async-start | bytes 1572864 | tf_op jit(solution)/shard_map/while/body/eval_jaxpr/all_to_all | solution.py:145
  438.2 24.1 %all-to-all-start.1 = ((bf16[1,128,8,384]{3,2,0,1:T(8,128)(2,1)}), bf16[1,128,8,384]{3,2,0,1:T(8,128)(2,1)S(1)}, u32[]{:S(2)}, u32[]{:S(2)}) async-start(bf16[1,128,8,384]{3,2,0,1:T(8,128)(2,1)} %copy.76), calls=%async_computation.1 | async-start | bytes 1572864 | tf_op jit(solution)/shard_map/while/body/eval_jaxpr/all_to_all | solution.py:159
  480.2 51.2 %copy-start.1 = (bf16[128,128,8]{1,0,2:T(8,128)(2,1)}, bf16[128,128,8]{1,0,2:T(8,128)(2,1)S(1)}, u32[]{:S(2)}) copy-start(bf16[128,128,8]{1,0,2:T(8,128)(2,1)S(1)} %get-tuple-element.1294) | copy-start | bytes 786436 | tf_op jit(solution)/shard_map/while
  480.3 21.4 %collective-permute-start = (bf16[1,8,256,192]{2,3,1,0:T(8,128)(2,1)S(1)}, bf16[1,8,256,192]{2,3,1,0:T(8,128)(2,1)S(1)}, u32[]{:S(2)}, u32[]{:S(2)}) collective-permute-start(bf16[1,8,256,192]{2,3,1,0:T(8,128)(2,1)S(1)} %broadcast_select_fusion.2), channel_id=1, source_target_pairs={{0,16},{1,17},{2,18},{3,19},{4,20},{5,21},{6,22},{7,23},{8,24},{9,... | collective-permute-start | bytes 2359304 | tf_op jit(solution)/shard_map/while/body/eval_jaxpr/ppermute | solution.py:17
  506.1 24.4 %all-to-all-start = ((bf16[1,8,128,384]{3,1,0,2:T(8,128)(2,1)}), bf16[1,8,128,384]{3,1,0,2:T(8,128)(2,1)S(1)}, u32[]{:S(2)}, u32[]{:S(2)}) async-start(bf16[1,8,128,384]{3,1,0,2:T(8,128)(2,1)} %copy.73), calls=%async_computation | async-start | bytes 1572864 | tf_op jit(solution)/shard_map/while/body/eval_jaxpr/all_to_all | solution.py:145
  533.2 24.1 %all-to-all-start.1 = ((bf16[1,128,8,384]{3,2,0,1:T(8,128)(2,1)}), bf16[1,128,8,384]{3,2,0,1:T(8,128)(2,1)S(1)}, u32[]{:S(2)}, u32[]{:S(2)}) async-start(bf16[1,128,8,384]{3,2,0,1:T(8,128)(2,1)} %copy.76), calls=%async_computation.1 | async-start | bytes 1572864 | tf_op jit(solution)/shard_map/while/body/eval_jaxpr/all_to_all | solution.py:159
  575.2 51.2 %copy-start.1 = (bf16[128,128,8]{1,0,2:T(8,128)(2,1)}, bf16[128,128,8]{1,0,2:T(8,128)(2,1)S(1)}, u32[]{:S(2)}) copy-start(bf16[128,128,8]{1,0,2:T(8,128)(2,1)S(1)} %get-tuple-element.1294) | copy-start | bytes 786436 | tf_op jit(solution)/shard_map/while
  575.3 21.4 %collective-permute-start = (bf16[1,8,256,192]{2,3,1,0:T(8,128)(2,1)S(1)}, bf16[1,8,256,192]{2,3,1,0:T(8,128)(2,1)S(1)}, u32[]{:S(2)}, u32[]{:S(2)}) collective-permute-start(bf16[1,8,256,192]{2,3,1,0:T(8,128)(2,1)S(1)} %broadcast_select_fusion.2), channel_id=1, source_target_pairs={{0,16},{1,17},{2,18},{3,19},{4,20},{5,21},{6,22},{7,23},{8,24},{9,... | collective-permute-start | bytes 2359304 | tf_op jit(solution)/shard_map/while/body/eval_jaxpr/ppermute | solution.py:17
  601.1 24.4 %all-to-all-start = ((bf16[1,8,128,384]{3,1,0,2:T(8,128)(2,1)}), bf16[1,8,128,384]{3,1,0,2:T(8,128)(2,1)S(1)}, u32[]{:S(2)}, u32[]{:S(2)}) async-start(bf16[1,8,128,384]{3,1,0,2:T(8,128)(2,1)} %copy.73), calls=%async_computation | async-start | bytes 1572864 | tf_op jit(solution)/shard_map/while/body/eval_jaxpr/all_to_all | solution.py:145
  628.2 24.1 %all-to-all-start.1 = ((bf16[1,128,8,384]{3,2,0,1:T(8,128)(2,1)}), bf16[1,128,8,384]{3,2,0,1:T(8,128)(2,1)S(1)}, u32[]{:S(2)}, u32[]{:S(2)}) async-start(bf16[1,128,8,384]{3,2,0,1:T(8,128)(2,1)} %copy.76), calls=%async_computation.1 | async-start | bytes 1572864 | tf_op jit(solution)/shard_map/while/body/eval_jaxpr/all_to_all | solution.py:159
  670.3 51.2 %copy-start.1 = (bf16[128,128,8]{1,0,2:T(8,128)(2,1)}, bf16[128,128,8]{1,0,2:T(8,128)(2,1)S(1)}, u32[]{:S(2)}) copy-start(bf16[128,128,8]{1,0,2:T(8,128)(2,1)S(1)} %get-tuple-element.1294) | copy-start | bytes 786436 | tf_op jit(solution)/shard_map/while
  670.3 21.4 %collective-permute-start = (bf16[1,8,256,192]{2,3,1,0:T(8,128)(2,1)S(1)}, bf16[1,8,256,192]{2,3,1,0:T(8,128)(2,1)S(1)}, u32[]{:S(2)}, u32[]{:S(2)}) collective-permute-start(bf16[1,8,256,192]{2,3,1,0:T(8,128)(2,1)S(1)} %broadcast_select_fusion.2), channel_id=1, source_target_pairs={{0,16},{1,17},{2,18},{3,19},{4,20},{5,21},{6,22},{7,23},{8,24},{9,... | collective-permute-start | bytes 2359304 | tf_op jit(solution)/shard_map/while/body/eval_jaxpr/ppermute | solution.py:17
  696.1 24.4 %all-to-all-start = ((bf16[1,8,128,384]{3,1,0,2:T(8,128)(2,1)}), bf16[1,8,128,384]{3,1,0,2:T(8,128)(2,1)S(1)}, u32[]{:S(2)}, u32[]{:S(2)}) async-start(bf16[1,8,128,384]{3,1,0,2:T(8,128)(2,1)} %copy.73), calls=%async_computation | async-start | bytes 1572864 | tf_op jit(solution)/shard_map/while/body/eval_jaxpr/all_to_all | solution.py:145
  723.2 24.1 %all-to-all-start.1 = ((bf16[1,128,8,384]{3,2,0,1:T(8,128)(2,1)}), bf16[1,128,8,384]{3,2,0,1:T(8,128)(2,1)S(1)}, u32[]{:S(2)}, u32[]{:S(2)}) async-start(bf16[1,128,8,384]{3,2,0,1:T(8,128)(2,1)} %copy.76), calls=%async_computation.1 | async-start | bytes 1572864 | tf_op jit(solution)/shard_map/while/body/eval_jaxpr/all_to_all | solution.py:159
  765.3 51.2 %copy-start.1 = (bf16[128,128,8]{1,0,2:T(8,128)(2,1)}, bf16[128,128,8]{1,0,2:T(8,128)(2,1)S(1)}, u32[]{:S(2)}) copy-start(bf16[128,128,8]{1,0,2:T(8,128)(2,1)S(1)} %get-tuple-element.1294) | copy-start | bytes 786436 | tf_op jit(solution)/shard_map/while
  765.3 21.4 %collective-permute-start = (bf16[1,8,256,192]{2,3,1,0:T(8,128)(2,1)S(1)}, bf16[1,8,256,192]{2,3,1,0:T(8,128)(2,1)S(1)}, u32[]{:S(2)}, u32[]{:S(2)}) collective-permute-start(bf16[1,8,256,192]{2,3,1,0:T(8,128)(2,1)S(1)} %broadcast_select_fusion.2), channel_id=1, source_target_pairs={{0,16},{1,17},{2,18},{3,19},{4,20},{5,21},{6,22},{7,23},{8,24},{9,... | collective-permute-start | bytes 2359304 | tf_op jit(solution)/shard_map/while/body/eval_jaxpr/ppermute | solution.py:17
  791.1 24.4 %all-to-all-start = ((bf16[1,8,128,384]{3,1,0,2:T(8,128)(2,1)}), bf16[1,8,128,384]{3,1,0,2:T(8,128)(2,1)S(1)}, u32[]{:S(2)}, u32[]{:S(2)}) async-start(bf16[1,8,128,384]{3,1,0,2:T(8,128)(2,1)} %copy.73), calls=%async_computation | async-start | bytes 1572864 | tf_op jit(solution)/shard_map/while/body/eval_jaxpr/all_to_all | solution.py:145
  818.2 24.1 %all-to-all-start.1 = ((bf16[1,128,8,384]{3,2,0,1:T(8,128)(2,1)}), bf16[1,128,8,384]{3,2,0,1:T(8,128)(2,1)S(1)}, u32[]{:S(2)}, u32[]{:S(2)}) async-start(bf16[1,128,8,384]{3,2,0,1:T(8,128)(2,1)} %copy.76), calls=%async_computation.1 | async-start | bytes 1572864 | tf_op jit(solution)/shard_map/while/body/eval_jaxpr/all_to_all | solution.py:159
  860.3 51.2 %copy-start.1 = (bf16[128,128,8]{1,0,2:T(8,128)(2,1)}, bf16[128,128,8]{1,0,2:T(8,128)(2,1)S(1)}, u32[]{:S(2)}) copy-start(bf16[128,128,8]{1,0,2:T(8,128)(2,1)S(1)} %get-tuple-element.1294) | copy-start | bytes 786436 | tf_op jit(solution)/shard_map/while
  860.4 21.4 %collective-permute-start = (bf16[1,8,256,192]{2,3,1,0:T(8,128)(2,1)S(1)}, bf16[1,8,256,192]{2,3,1,0:T(8,128)(2,1)S(1)}, u32[]{:S(2)}, u32[]{:S(2)}) collective-permute-start(bf16[1,8,256,192]{2,3,1,0:T(8,128)(2,1)S(1)} %broadcast_select_fusion.2), channel_id=1, source_target_pairs={{0,16},{1,17},{2,18},{3,19},{4,20},{5,21},{6,22},{7,23},{8,24},{9,... | collective-permute-start | bytes 2359304 | tf_op jit(solution)/shard_map/while/body/eval_jaxpr/ppermute | solution.py:17
  886.1 24.4 %all-to-all-start = ((bf16[1,8,128,384]{3,1,0,2:T(8,128)(2,1)}), bf16[1,8,128,384]{3,1,0,2:T(8,128)(2,1)S(1)}, u32[]{:S(2)}, u32[]{:S(2)}) async-start(bf16[1,8,128,384]{3,1,0,2:T(8,128)(2,1)} %copy.73), calls=%async_computation | async-start | bytes 1572864 | tf_op jit(solution)/shard_map/while/body/eval_jaxpr/all_to_all | solution.py:145
  913.3 24.1 %all-to-all-start.1 = ((bf16[1,128,8,384]{3,2,0,1:T(8,128)(2,1)}), bf16[1,128,8,384]{3,2,0,1:T(8,128)(2,1)S(1)}, u32[]{:S(2)}, u32[]{:S(2)}) async-start(bf16[1,128,8,384]{3,2,0,1:T(8,128)(2,1)} %copy.76), calls=%async_computation.1 | async-start | bytes 1572864 | tf_op jit(solution)/shard_map/while/body/eval_jaxpr/all_to_all | solution.py:159
  (63 other events, 653.5 us)
Sparse Core Ops, SparseCore 0:
  10.2 71.5 all-gather.1
where the time goes:
time: 987 us; the launch traced here: 980 us
  waiting for transfers between devices  414 us (42%)
  other arithmetic  201 us (20%)
  matrix products  122 us (12%)
  loops' own time  83.8 us (8%)
  starting transfers between devices  76.3 us (8%)
  local copies, waits for them, and re-layouts  69.8 us (7%)
  between operations  13.6 us (1%)
    ppermute x7, waiting for transfers between devices, shifted_2(): lax.ppermute(value, axis, [(source, source + steps) for source in range(f...  140 us
    all_to_all x7, waiting for transfers between devices, spectral(): lax.all_to_all(returned, 'sht', split_axis=1, concat_axis=2, tiled=True)  137 us
    all_to_all x7, waiting for transfers between devices, spectral(): lax.all_to_all(spectrum, 'sht', split_axis=2, concat_axis=1, tiled=True)  137 us
    another operation x1, loops' own time, legendre_table(): lax.scan(advance, (initial, initial), jnp.arange(lmax, dtype=jnp.int32),...  81.8 us
    gt x128, other arithmetic, advance(): degree > m_index[None, :] + 1  78.8 us
    eq x64, other arithmetic, advance(): degree == m_index[None, :]  78.2 us
    dot_general x7, matrix products, sfno_block(): jnp.dot(second.reshape(-1, channels), mlp_in[0], preferred_element_type=j...  52.6 us
    all_to_all x7, starting transfers between devices, spectral(): lax.all_to_all(spectrum, 'sht', split_axis=2, concat_axis=1, tiled=True)  36.1 us
  transfers between devices with their start and end apart: 22, of which 21 were waited for; matrix products, arithmetic and copies ran while one was open for 19% of the time, Pallas kernels for 0%

commit v1 on v0

--- a/solution.py
+++ b/solution.py
@@ -142,7 +142,12 @@
             "bjkc,kpm->bjmpc", normed, forward, preferred_element_type=jnp.float32
         ).astype(jnp.bfloat16)
         spectrum = spectrum.reshape(batch_rows, lat_rows, MMAX, 2 * C)
-        exchanged = lax.all_to_all(spectrum, "sht", split_axis=2, concat_axis=1, tiled=True)
+        exchanged = jnp.concatenate(
+            lax.all_to_all(
+                jnp.stack(jnp.split(spectrum, lax.axis_size("sht"), axis=2)), "sht", 0, 0
+            ),
+            axis=1,
+        )
         item_count = exchanged.shape[0]
         coeffs = jnp.einsum(
             "jlm,bjmq->blmq", weighted, exchanged, preferred_element_type=jnp.float32

time: 987 us -> 1290 us (1.31)
  local copies, waits for them, and re-layouts: 69.8 us -> 356 us
    while x147 -> x532, local copies, waits for them, and re-layouts: 10.8 us -> 264 us
    split x0 -> x7, local copies, waits for them, and re-layouts: none -> 39 us  [spectral(): jnp.split(spectrum, lax.axis_size('sht'), axis=2)]
  transfers between devices with their start and end apart: 22 -> 22, of which waited for: 21 -> 21; matrix products, arithmetic and copies ran while one was open for 19% -> 15% of each run, Pallas kernels for 0% -> 0%
where the time goes in v1:
time: 1290 us; the launch traced here: 1280 us
  waiting for transfers between devices  414 us (32%)
  local copies, waits for them, and re-layouts  356 us (28%)
  other arithmetic  213 us (17%)
  matrix products  117 us (9%)
  loops' own time  87.3 us (7%)
  starting transfers between devices  76.3 us (6%)
  between operations  13.6 us (1%)
    while x532, local copies, waits for them, and re-layouts  264 us
    ppermute x7, waiting for transfers between devices, shifted_2(): lax.ppermute(value, axis, [(source, source + steps) for source in range(f...  140 us
    all_to_all x7, waiting for transfers between devices, spectral(): lax.all_to_all(returned, 'sht', split_axis=1, concat_axis=2, tiled=True)  137 us
    all_to_all x7, waiting for transfers between devices, spectral(): lax.all_to_all(jnp.stack(jnp.split(spectrum, lax.axis_size('sht'), axis=2...  137 us
    another operation x1, loops' own time, legendre_table(): lax.scan(advance, (initial, initial), jnp.arange(lmax, dtype=jnp.int32),...  84.9 us
    gt x128, other arithmetic, advance(): degree > m_index[None, :] + 1  81 us
    eq x64, other arithmetic, advance(): degree == m_index[None, :]  80.6 us
    dot_general x7, matrix products, sfno_block(): jnp.dot(second.reshape(-1, channels), mlp_in[0], preferred_element_type=j...  52.6 us
  transfers between devices with their start and end apart: 22, of which 21 were waited for; matrix products, arithmetic and copies ran while one was open for 15% of the time, Pallas kernels for 0%

profile of v1, /device:TPU:11, one launch (start us, length us, event | category | flops | bytes accessed | tf_op | source)
XLA Modules:
  0.0 1277.4 jit_solution(17573320638909009819)
XLA Ops:
  10.8 271.4 %while.39 = (s32[]{:T(128)}, f32[128,8]{0,1:T(8,128)S(1)}, f32[128,8]{0,1:T(8,128)S(1)}, f32[16,8,128,8]{2,3,1,0:T(8,128)S(1)}, s32[16,8]{0,1:T(8,128)S(1)}, /*i...) while((s32[]{:T(128)}, f32[128,8]{0,1:T(8,128)S(1)}, ...), condition=%wide.region_4.5_spmd.clone.clone.clone.clone, body=%wide.region_3.4_spmd.clone.clone.clone.clone.sunk | while | flops 102682 | bytes 236484 | solution.py:67
  297.3 955.0 %while.38 = (s32[]{:T(128)}, bf16[1,8,256,192]{2,3,1,0:T(8,128)(2,1)}, bf16[6,8,256,192]{2,3,1,0:T(8,128)(2,1)}, pred[]{:T(512)}, bf16[6,8,256,192]{2,3,1,0:T(8,...) while((s32[]{:T(128)}, ...), condition=%wide.region_10.11_spmd.clone, body=%wide.region_5.10_spmd.clone.sunk | while | flops 1450184704 | bytes 58836228 | solution.py:207
  298.7 19.0 %collective-permute-done = bf16[1,8,256,192]{2,3,1,0:T(8,128)(2,1)S(1)} collective-permute-done((bf16[1,8,256,192]{2,3,1,0:T(8,128)(2,1)S(1)}, bf16[1,8,256,192]{2,3,1,0:T(8,128)(2,1)S(1)}, u32[]{:S(2)}, u32[]{:S(2)}) %collective-permute-start) | collective-permute-done | bytes 786464 | tf_op jit(solution)/shard_map/while/body/eval_jaxpr/ppermute | solution.py:17
  369.8 19.6 %all-to-all-done = bf16[16,1,8,8,384]{4,3,2,1,0:T(8,128)(2,1)S(1)} async-done(((bf16[16,1,8,8,384]{4,3,2,1,0:T(8,128)(2,1)}), bf16[16,1,8,8,384]{4,3,2,1,0:T(8,128)(2,1)S(1)}, u32[]{:S(2)}, u32[]{:S(2)}) %all-to-all-start) | async-done | bytes 786464 | tf_op jit(solution)/shard_map/while/body/eval_jaxpr/all_to_all | solution.py:146
  396.2 19.6 %all-to-all-done.1 = bf16[1,128,8,384]{3,2,0,1:T(8,128)(2,1)S(1)} async-done(((bf16[1,128,8,384]{3,2,0,1:T(8,128)(2,1)}), bf16[1,128,8,384]{3,2,0,1:T(8,128)(2,1)S(1)}, u32[]{:S(2)}, u32[]{:S(2)}) %all-to-all-start.1) | async-done | bytes 786464 | tf_op jit(solution)/shard_map/while/body/eval_jaxpr/all_to_all | solution.py:164
  423.4 7.5 fusion.156
  436.6 20.1 %collective-permute-done = bf16[1,8,256,192]{2,3,1,0:T(8,128)(2,1)S(1)} collective-permute-done((bf16[1,8,256,192]{2,3,1,0:T(8,128)(2,1)S(1)}, bf16[1,8,256,192]{2,3,1,0:T(8,128)(2,1)S(1)}, u32[]{:S(2)}, u32[]{:S(2)}) %collective-permute-start) | collective-permute-done | bytes 786464 | tf_op jit(solution)/shard_map/while/body/eval_jaxpr/ppermute | solution.py:17
  506.1 19.6 %all-to-all-done = bf16[16,1,8,8,384]{4,3,2,1,0:T(8,128)(2,1)S(1)} async-done(((bf16[16,1,8,8,384]{4,3,2,1,0:T(8,128)(2,1)}), bf16[16,1,8,8,384]{4,3,2,1,0:T(8,128)(2,1)S(1)}, u32[]{:S(2)}, u32[]{:S(2)}) %all-to-all-start) | async-done | bytes 786464 | tf_op jit(solution)/shard_map/while/body/eval_jaxpr/all_to_all | solution.py:146
  532.6 19.6 %all-to-all-done.1 = bf16[1,128,8,384]{3,2,0,1:T(8,128)(2,1)S(1)} async-done(((bf16[1,128,8,384]{3,2,0,1:T(8,128)(2,1)}), bf16[1,128,8,384]{3,2,0,1:T(8,128)(2,1)S(1)}, u32[]{:S(2)}, u32[]{:S(2)}) %all-to-all-start.1) | async-done | bytes 786464 | tf_op jit(solution)/shard_map/while/body/eval_jaxpr/all_to_all | solution.py:164
  559.8 7.5 fusion.156
  573.0 20.1 %collective-permute-done = bf16[1,8,256,192]{2,3,1,0:T(8,128)(2,1)S(1)} collective-permute-done((bf16[1,8,256,192]{2,3,1,0:T(8,128)(2,1)S(1)}, bf16[1,8,256,192]{2,3,1,0:T(8,128)(2,1)S(1)}, u32[]{:S(2)}, u32[]{:S(2)}) %collective-permute-start) | collective-permute-done | bytes 786464 | tf_op jit(solution)/shard_map/while/body/eval_jaxpr/ppermute | solution.py:17
  642.5 19.6 %all-to-all-done = bf16[16,1,8,8,384]{4,3,2,1,0:T(8,128)(2,1)S(1)} async-done(((bf16[16,1,8,8,384]{4,3,2,1,0:T(8,128)(2,1)}), bf16[16,1,8,8,384]{4,3,2,1,0:T(8,128)(2,1)S(1)}, u32[]{:S(2)}, u32[]{:S(2)}) %all-to-all-start) | async-done | bytes 786464 | tf_op jit(solution)/shard_map/while/body/eval_jaxpr/all_to_all | solution.py:146
  669.0 19.6 %all-to-all-done.1 = bf16[1,128,8,384]{3,2,0,1:T(8,128)(2,1)S(1)} async-done(((bf16[1,128,8,384]{3,2,0,1:T(8,128)(2,1)}), bf16[1,128,8,384]{3,2,0,1:T(8,128)(2,1)S(1)}, u32[]{:S(2)}, u32[]{:S(2)}) %all-to-all-start.1) | async-done | bytes 786464 | tf_op jit(solution)/shard_map/while/body/eval_jaxpr/all_to_all | solution.py:164
  696.2 7.5 fusion.156
  709.4 20.1 %collective-permute-done = bf16[1,8,256,192]{2,3,1,0:T(8,128)(2,1)S(1)} collective-permute-done((bf16[1,8,256,192]{2,3,1,0:T(8,128)(2,1)S(1)}, bf16[1,8,256,192]{2,3,1,0:T(8,128)(2,1)S(1)}, u32[]{:S(2)}, u32[]{:S(2)}) %collective-permute-start) | collective-permute-done | bytes 786464 | tf_op jit(solution)/shard_map/while/body/eval_jaxpr/ppermute | solution.py:17
  778.9 19.6 %all-to-all-done = bf16[16,1,8,8,384]{4,3,2,1,0:T(8,128)(2,1)S(1)} async-done(((bf16[16,1,8,8,384]{4,3,2,1,0:T(8,128)(2,1)}), bf16[16,1,8,8,384]{4,3,2,1,0:T(8,128)(2,1)S(1)}, u32[]{:S(2)}, u32[]{:S(2)}) %all-to-all-start) | async-done | bytes 786464 | tf_op jit(solution)/shard_map/while/body/eval_jaxpr/all_to_all | solution.py:146
  805.4 19.6 %all-to-all-done.1 = bf16[1,128,8,384]{3,2,0,1:T(8,128)(2,1)S(1)} async-done(((bf16[1,128,8,384]{3,2,0,1:T(8,128)(2,1)}), bf16[1,128,8,384]{3,2,0,1:T(8,128)(2,1)S(1)}, u32[]{:S(2)}, u32[]{:S(2)}) %all-to-all-start.1) | async-done | bytes 786464 | tf_op jit(solution)/shard_map/while/body/eval_jaxpr/all_to_all | solution.py:164
  832.6 7.5 fusion.156
  845.8 20.1 %collective-permute-done = bf16[1,8,256,192]{2,3,1,0:T(8,128)(2,1)S(1)} collective-permute-done((bf16[1,8,256,192]{2,3,1,0:T(8,128)(2,1)S(1)}, bf16[1,8,256,192]{2,3,1,0:T(8,128)(2,1)S(1)}, u32[]{:S(2)}, u32[]{:S(2)}) %collective-permute-start) | collective-permute-done | bytes 786464 | tf_op jit(solution)/shard_map/while/body/eval_jaxpr/ppermute | solution.py:17
  915.3 19.6 %all-to-all-done = bf16[16,1,8,8,384]{4,3,2,1,0:T(8,128)(2,1)S(1)} async-done(((bf16[16,1,8,8,384]{4,3,2,1,0:T(8,128)(2,1)}), bf16[16,1,8,8,384]{4,3,2,1,0:T(8,128)(2,1)S(1)}, u32[]{:S(2)}, u32[]{:S(2)}) %all-to-all-start) | async-done | bytes 786464 | tf_op jit(solution)/shard_map/while/body/eval_jaxpr/all_to_all | solution.py:146
  941.8 19.6 %all-to-all-done.1 = bf16[1,128,8,384]{3,2,0,1:T(8,128)(2,1)S(1)} async-done(((bf16[1,128,8,384]{3,2,0,1:T(8,128)(2,1)}), bf16[1,128,8,384]{3,2,0,1:T(8,128)(2,1)S(1)}, u32[]{:S(2)}, u32[]{:S(2)}) %all-to-all-start.1) | async-done | bytes 786464 | tf_op jit(solution)/shard_map/while/body/eval_jaxpr/all_to_all | solution.py:164
  968.9 7.5 fusion.156
  982.1 20.1 %collective-permute-done = bf16[1,8,256,192]{2,3,1,0:T(8,128)(2,1)S(1)} collective-permute-done((bf16[1,8,256,192]{2,3,1,0:T(8,128)(2,1)S(1)}, bf16[1,8,256,192]{2,3,1,0:T(8,128)(2,1)S(1)}, u32[]{:S(2)}, u32[]{:S(2)}) %collective-permute-start) | collective-permute-done | bytes 786464 | tf_op jit(solution)/shard_map/while/body/eval_jaxpr/ppermute | solution.py:17
  1051.6 19.6 %all-to-all-done = bf16[16,1,8,8,384]{4,3,2,1,0:T(8,128)(2,1)S(1)} async-done(((bf16[16,1,8,8,384]{4,3,2,1,0:T(8,128)(2,1)}), bf16[16,1,8,8,384]{4,3,2,1,0:T(8,128)(2,1)S(1)}, u32[]{:S(2)}, u32[]{:S(2)}) %all-to-all-start) | async-done | bytes 786464 | tf_op jit(solution)/shard_map/while/body/eval_jaxpr/all_to_all | solution.py:146
  1078.1 19.6 %all-to-all-done.1 = bf16[1,128,8,384]{3,2,0,1:T(8,128)(2,1)S(1)} async-done(((bf16[1,128,8,384]{3,2,0,1:T(8,128)(2,1)}), bf16[1,128,8,384]{3,2,0,1:T(8,128)(2,1)S(1)}, u32[]{:S(2)}, u32[]{:S(2)}) %all-to-all-start.1) | async-done | bytes 786464 | tf_op jit(solution)/shard_map/while/body/eval_jaxpr/all_to_all | solution.py:164
  1105.3 7.5 fusion.156
  1118.5 20.1 %collective-permute-done = bf16[1,8,256,192]{2,3,1,0:T(8,128)(2,1)S(1)} collective-permute-done((bf16[1,8,256,192]{2,3,1,0:T(8,128)(2,1)S(1)}, bf16[1,8,256,192]{2,3,1,0:T(8,128)(2,1)S(1)}, u32[]{:S(2)}, u32[]{:S(2)}) %collective-permute-start) | collective-permute-done | bytes 786464 | tf_op jit(solution)/shard_map/while/body/eval_jaxpr/ppermute | solution.py:17
  1188.0 19.6 %all-to-all-done = bf16[16,1,8,8,384]{4,3,2,1,0:T(8,128)(2,1)S(1)} async-done(((bf16[16,1,8,8,384]{4,3,2,1,0:T(8,128)(2,1)}), bf16[16,1,8,8,384]{4,3,2,1,0:T(8,128)(2,1)S(1)}, u32[]{:S(2)}, u32[]{:S(2)}) %all-to-all-start) | async-done | bytes 786464 | tf_op jit(solution)/shard_map/while/body/eval_jaxpr/all_to_all | solution.py:146
  1214.5 19.6 %all-to-all-done.1 = bf16[1,128,8,384]{3,2,0,1:T(8,128)(2,1)S(1)} async-done(((bf16[1,128,8,384]{3,2,0,1:T(8,128)(2,1)}), bf16[1,128,8,384]{3,2,0,1:T(8,128)(2,1)S(1)}, u32[]{:S(2)}, u32[]{:S(2)}) %all-to-all-start.1) | async-done | bytes 786464 | tf_op jit(solution)/shard_map/while/body/eval_jaxpr/all_to_all | solution.py:164
  1241.7 7.5 fusion.156
  1252.3 8.0 copy.92
  1260.3 10.2 broadcast_in_dim_reshape.3
  (1282 shorter events, 691.8 us)
Async XLA Ops:
  6.5 280.3 %all-gather.2.cloned.1.call-start = ((), (), s32[]{:S(2)}) async-start(), calls=%async_computation.2 | async-start | bytes 8257536 | tf_op jit(solution)/shard_map/all_gather | solution.py:127
  10.7 271.7 %copy-start.17 = (f32[1,2,24576]{2,1,0:T(2,128)S(1)}, f32[1,2,24576]{2,1,0:T(2,128)}, u32[]{:S(2)}) copy-start(f32[1,2,24576]{2,1,0:T(2,128)} %param.15) | copy-start | bytes 589828
  297.4 20.3 %collective-permute-start = (bf16[1,8,256,192]{2,3,1,0:T(8,128)(2,1)S(1)}, bf16[1,8,256,192]{2,3,1,0:T(8,128)(2,1)S(1)}, u32[]{:S(2)}, u32[]{:S(2)}) collective-permute-start(bf16[1,8,256,192]{2,3,1,0:T(8,128)(2,1)S(1)} %broadcast_select_fusion.2), channel_id=1, source_target_pairs={{0,16},{1,17},{2,18},{3,19},{4,20},{5,21},{6,22},{7,23},{8,24},{9,... | collective-permute-start | bytes 2359304 | tf_op jit(solution)/shard_map/while/body/eval_jaxpr/ppermute | solution.py:17
  353.2 36.2 %copy-start.1 = (bf16[128,128,8]{1,0,2:T(8,128)(2,1)S(1)}, bf16[128,128,8]{1,0,2:T(8,128)(2,1)}, u32[]{:S(2)}) copy-start(bf16[128,128,8]{1,0,2:T(8,128)(2,1)} %get-tuple-element.1340) | copy-start | bytes 786436 | tf_op jit(solution)/shard_map/while
  362.3 27.0 %all-to-all-start = ((bf16[16,1,8,8,384]{4,3,2,1,0:T(8,128)(2,1)}), bf16[16,1,8,8,384]{4,3,2,1,0:T(8,128)(2,1)S(1)}, u32[]{:S(2)}, u32[]{:S(2)}) async-start(bf16[16,1,8,8,384]{4,3,2,1,0:T(8,128)(2,1)} %bitcast_dynamic-update-slice_fusion.49), calls=%async_computation | async-start | bytes 1572864 | tf_op jit(solution)/shard_map/while/body/eval_jaxpr/all_to_all | solution.py:146
  391.8 24.1 %all-to-all-start.1 = ((bf16[1,128,8,384]{3,2,0,1:T(8,128)(2,1)}), bf16[1,128,8,384]{3,2,0,1:T(8,128)(2,1)S(1)}, u32[]{:S(2)}, u32[]{:S(2)}) async-start(bf16[1,128,8,384]{3,2,0,1:T(8,128)(2,1)} %copy.156), calls=%async_computation.1 | async-start | bytes 1572864 | tf_op jit(solution)/shard_map/while/body/eval_jaxpr/all_to_all | solution.py:164
  435.3 21.4 %collective-permute-start = (bf16[1,8,256,192]{2,3,1,0:T(8,128)(2,1)S(1)}, bf16[1,8,256,192]{2,3,1,0:T(8,128)(2,1)S(1)}, u32[]{:S(2)}, u32[]{:S(2)}) collective-permute-start(bf16[1,8,256,192]{2,3,1,0:T(8,128)(2,1)S(1)} %broadcast_select_fusion.2), channel_id=1, source_target_pairs={{0,16},{1,17},{2,18},{3,19},{4,20},{5,21},{6,22},{7,23},{8,24},{9,... | collective-permute-start | bytes 2359304 | tf_op jit(solution)/shard_map/while/body/eval_jaxpr/ppermute | solution.py:17
  492.2 33.5 %copy-start.1 = (bf16[128,128,8]{1,0,2:T(8,128)(2,1)S(1)}, bf16[128,128,8]{1,0,2:T(8,128)(2,1)}, u32[]{:S(2)}) copy-start(bf16[128,128,8]{1,0,2:T(8,128)(2,1)} %get-tuple-element.1340) | copy-start | bytes 786436 | tf_op jit(solution)/shard_map/while
  501.3 24.4 %all-to-all-start = ((bf16[16,1,8,8,384]{4,3,2,1,0:T(8,128)(2,1)}), bf16[16,1,8,8,384]{4,3,2,1,0:T(8,128)(2,1)S(1)}, u32[]{:S(2)}, u32[]{:S(2)}) async-start(bf16[16,1,8,8,384]{4,3,2,1,0:T(8,128)(2,1)} %bitcast_dynamic-update-slice_fusion.49), calls=%async_computation | async-start | bytes 1572864 | tf_op jit(solution)/shard_map/while/body/eval_jaxpr/all_to_all | solution.py:146
  528.2 24.1 %all-to-all-start.1 = ((bf16[1,128,8,384]{3,2,0,1:T(8,128)(2,1)}), bf16[1,128,8,384]{3,2,0,1:T(8,128)(2,1)S(1)}, u32[]{:S(2)}, u32[]{:S(2)}) async-start(bf16[1,128,8,384]{3,2,0,1:T(8,128)(2,1)} %copy.156), calls=%async_computation.1 | async-start | bytes 1572864 | tf_op jit(solution)/shard_map/while/body/eval_jaxpr/all_to_all | solution.py:164
  570.5 24.3 %copy-start.18 = (bf16[256,2,128]{2,0,1:T(8,128)(2,1)}, bf16[256,2,128]{2,0,1:T(8,128)(2,1)S(1)}, u32[]{:S(2)}) copy-start(bf16[256,2,128]{2,0,1:T(8,128)(2,1)S(1)} %get-tuple-element.1339) | copy-start | bytes 393220 | tf_op jit(solution)/shard_map/while
  571.7 21.4 %collective-permute-start = (bf16[1,8,256,192]{2,3,1,0:T(8,128)(2,1)S(1)}, bf16[1,8,256,192]{2,3,1,0:T(8,128)(2,1)S(1)}, u32[]{:S(2)}, u32[]{:S(2)}) collective-permute-start(bf16[1,8,256,192]{2,3,1,0:T(8,128)(2,1)S(1)} %broadcast_select_fusion.2), channel_id=1, source_target_pairs={{0,16},{1,17},{2,18},{3,19},{4,20},{5,21},{6,22},{7,23},{8,24},{9,... | collective-permute-start | bytes 2359304 | tf_op jit(solution)/shard_map/while/body/eval_jaxpr/ppermute | solution.py:17
  628.6 33.5 %copy-start.1 = (bf16[128,128,8]{1,0,2:T(8,128)(2,1)S(1)}, bf16[128,128,8]{1,0,2:T(8,128)(2,1)}, u32[]{:S(2)}) copy-start(bf16[128,128,8]{1,0,2:T(8,128)(2,1)} %get-tuple-element.1340) | copy-start | bytes 786436 | tf_op jit(solution)/shard_map/while
  637.7 24.4 %all-to-all-start = ((bf16[16,1,8,8,384]{4,3,2,1,0:T(8,128)(2,1)}), bf16[16,1,8,8,384]{4,3,2,1,0:T(8,128)(2,1)S(1)}, u32[]{:S(2)}, u32[]{:S(2)}) async-start(bf16[16,1,8,8,384]{4,3,2,1,0:T(8,128)(2,1)} %bitcast_dynamic-update-slice_fusion.49), calls=%async_computation | async-start | bytes 1572864 | tf_op jit(solution)/shard_map/while/body/eval_jaxpr/all_to_all | solution.py:146
  664.6 24.1 %all-to-all-start.1 = ((bf16[1,128,8,384]{3,2,0,1:T(8,128)(2,1)}), bf16[1,128,8,384]{3,2,0,1:T(8,128)(2,1)S(1)}, u32[]{:S(2)}, u32[]{:S(2)}) async-start(bf16[1,128,8,384]{3,2,0,1:T(8,128)(2,1)} %copy.156), calls=%async_computation.1 | async-start | bytes 1572864 | tf_op jit(solution)/shard_map/while/body/eval_jaxpr/all_to_all | solution.py:164
  706.8 24.3 %copy-start.18 = (bf16[256,2,128]{2,0,1:T(8,128)(2,1)}, bf16[256,2,128]{2,0,1:T(8,128)(2,1)S(1)}, u32[]{:S(2)}) copy-start(bf16[256,2,128]{2,0,1:T(8,128)(2,1)S(1)} %get-tuple-element.1339) | copy-start | bytes 393220 | tf_op jit(solution)/shard_map/while
  708.1 21.4 %collective-permute-start = (bf16[1,8,256,192]{2,3,1,0:T(8,128)(2,1)S(1)}, bf16[1,8,256,192]{2,3,1,0:T(8,128)(2,1)S(1)}, u32[]{:S(2)}, u32[]{:S(2)}) collective-permute-start(bf16[1,8,256,192]{2,3,1,0:T(8,128)(2,1)S(1)} %broadcast_select_fusion.2), channel_id=1, source_target_pairs={{0,16},{1,17},{2,18},{3,19},{4,20},{5,21},{6,22},{7,23},{8,24},{9,... | collective-permute-start | bytes 2359304 | tf_op jit(solution)/shard_map/while/body/eval_jaxpr/ppermute | solution.py:17
  764.9 33.5 %copy-start.1 = (bf16[128,128,8]{1,0,2:T(8,128)(2,1)S(1)}, bf16[128,128,8]{1,0,2:T(8,128)(2,1)}, u32[]{:S(2)}) copy-start(bf16[128,128,8]{1,0,2:T(8,128)(2,1)} %get-tuple-element.1340) | copy-start | bytes 786436 | tf_op jit(solution)/shard_map/while
  774.1 24.4 %all-to-all-start = ((bf16[16,1,8,8,384]{4,3,2,1,0:T(8,128)(2,1)}), bf16[16,1,8,8,384]{4,3,2,1,0:T(8,128)(2,1)S(1)}, u32[]{:S(2)}, u32[]{:S(2)}) async-start(bf16[16,1,8,8,384]{4,3,2,1,0:T(8,128)(2,1)} %bitcast_dynamic-update-slice_fusion.49), calls=%async_computation | async-start | bytes 1572864 | tf_op jit(solution)/shard_map/while/body/eval_jaxpr/all_to_all | solution.py:146
  800.9 24.1 %all-to-all-start.1 = ((bf16[1,128,8,384]{3,2,0,1:T(8,128)(2,1)}), bf16[1,128,8,384]{3,2,0,1:T(8,128)(2,1)S(1)}, u32[]{:S(2)}, u32[]{:S(2)}) async-start(bf16[1,128,8,384]{3,2,0,1:T(8,128)(2,1)} %copy.156), calls=%async_computation.1 | async-start | bytes 1572864 | tf_op jit(solution)/shard_map/while/body/eval_jaxpr/all_to_all | solution.py:164
  844.5 21.4 %collective-permute-start = (bf16[1,8,256,192]{2,3,1,0:T(8,128)(2,1)S(1)}, bf16[1,8,256,192]{2,3,1,0:T(8,128)(2,1)S(1)}, u32[]{:S(2)}, u32[]{:S(2)}) collective-permute-start(bf16[1,8,256,192]{2,3,1,0:T(8,128)(2,1)S(1)} %broadcast_select_fusion.2), channel_id=1, source_target_pairs={{0,16},{1,17},{2,18},{3,19},{4,20},{5,21},{6,22},{7,23},{8,24},{9,... | collective-permute-start | bytes 2359304 | tf_op jit(solution)/shard_map/while/body/eval_jaxpr/ppermute | solution.py:17
  901.3 33.5 %copy-start.1 = (bf16[128,128,8]{1,0,2:T(8,128)(2,1)S(1)}, bf16[128,128,8]{1,0,2:T(8,128)(2,1)}, u32[]{:S(2)}) copy-start(bf16[128,128,8]{1,0,2:T(8,128)(2,1)} %get-tuple-element.1340) | copy-start | bytes 786436 | tf_op jit(solution)/shard_map/while
  910.5 24.4 %all-to-all-start = ((bf16[16,1,8,8,384]{4,3,2,1,0:T(8,128)(2,1)}), bf16[16,1,8,8,384]{4,3,2,1,0:T(8,128)(2,1)S(1)}, u32[]{:S(2)}, u32[]{:S(2)}) async-start(bf16[16,1,8,8,384]{4,3,2,1,0:T(8,128)(2,1)} %bitcast_dynamic-update-slice_fusion.49), calls=%async_computation | async-start | bytes 1572864 | tf_op jit(solution)/shard_map/while/body/eval_jaxpr/all_to_all | solution.py:146
  937.3 24.1 %all-to-all-start.1 = ((bf16[1,128,8,384]{3,2,0,1:T(8,128)(2,1)}), bf16[1,128,8,384]{3,2,0,1:T(8,128)(2,1)S(1)}, u32[]{:S(2)}, u32[]{:S(2)}) async-start(bf16[1,128,8,384]{3,2,0,1:T(8,128)(2,1)} %copy.156), calls=%async_computation.1 | async-start | bytes 1572864 | tf_op jit(solution)/shard_map/while/body/eval_jaxpr/all_to_all | solution.py:164
  980.8 21.4 %collective-permute-start = (bf16[1,8,256,192]{2,3,1,0:T(8,128)(2,1)S(1)}, bf16[1,8,256,192]{2,3,1,0:T(8,128)(2,1)S(1)}, u32[]{:S(2)}, u32[]{:S(2)}) collective-permute-start(bf16[1,8,256,192]{2,3,1,0:T(8,128)(2,1)S(1)} %broadcast_select_fusion.2), channel_id=1, source_target_pairs={{0,16},{1,17},{2,18},{3,19},{4,20},{5,21},{6,22},{7,23},{8,24},{9,... | collective-permute-start | bytes 2359304 | tf_op jit(solution)/shard_map/while/body/eval_jaxpr/ppermute | solution.py:17
  1037.7 33.5 %copy-start.1 = (bf16[128,128,8]{1,0,2:T(8,128)(2,1)S(1)}, bf16[128,128,8]{1,0,2:T(8,128)(2,1)}, u32[]{:S(2)}) copy-start(bf16[128,128,8]{1,0,2:T(8,128)(2,1)} %get-tuple-element.1340) | copy-start | bytes 786436 | tf_op jit(solution)/shard_map/while
  1046.8 24.4 %all-to-all-start = ((bf16[16,1,8,8,384]{4,3,2,1,0:T(8,128)(2,1)}), bf16[16,1,8,8,384]{4,3,2,1,0:T(8,128)(2,1)S(1)}, u32[]{:S(2)}, u32[]{:S(2)}) async-start(bf16[16,1,8,8,384]{4,3,2,1,0:T(8,128)(2,1)} %bitcast_dynamic-update-slice_fusion.49), calls=%async_computation | async-start | bytes 1572864 | tf_op jit(solution)/shard_map/while/body/eval_jaxpr/all_to_all | solution.py:146
  1073.7 24.1 %all-to-all-start.1 = ((bf16[1,128,8,384]{3,2,0,1:T(8,128)(2,1)}), bf16[1,128,8,384]{3,2,0,1:T(8,128)(2,1)S(1)}, u32[]{:S(2)}, u32[]{:S(2)}) async-start(bf16[1,128,8,384]{3,2,0,1:T(8,128)(2,1)} %copy.156), calls=%async_computation.1 | async-start | bytes 1572864 | tf_op jit(solution)/shard_map/while/body/eval_jaxpr/all_to_all | solution.py:164
  1117.2 21.4 %collective-permute-start = (bf16[1,8,256,192]{2,3,1,0:T(8,128)(2,1)S(1)}, bf16[1,8,256,192]{2,3,1,0:T(8,128)(2,1)S(1)}, u32[]{:S(2)}, u32[]{:S(2)}) collective-permute-start(bf16[1,8,256,192]{2,3,1,0:T(8,128)(2,1)S(1)} %broadcast_select_fusion.2), channel_id=1, source_target_pairs={{0,16},{1,17},{2,18},{3,19},{4,20},{5,21},{6,22},{7,23},{8,24},{9,... | collective-permute-start | bytes 2359304 | tf_op jit(solution)/shard_map/while/body/eval_jaxpr/ppermute | solution.py:17
  1174.1 33.5 %copy-start.1 = (bf16[128,128,8]{1,0,2:T(8,128)(2,1)S(1)}, bf16[128,128,8]{1,0,2:T(8,128)(2,1)}, u32[]{:S(2)}) copy-start(bf16[128,128,8]{1,0,2:T(8,128)(2,1)} %get-tuple-element.1340) | copy-start | bytes 786436 | tf_op jit(solution)/shard_map/while
  1183.2 24.4 %all-to-all-start = ((bf16[16,1,8,8,384]{4,3,2,1,0:T(8,128)(2,1)}), bf16[16,1,8,8,384]{4,3,2,1,0:T(8,128)(2,1)S(1)}, u32[]{:S(2)}, u32[]{:S(2)}) async-start(bf16[16,1,8,8,384]{4,3,2,1,0:T(8,128)(2,1)} %bitcast_dynamic-update-slice_fusion.49), calls=%async_computation | async-start | bytes 1572864 | tf_op jit(solution)/shard_map/while/body/eval_jaxpr/all_to_all | solution.py:146
  1210.1 24.1 %all-to-all-start.1 = ((bf16[1,128,8,384]{3,2,0,1:T(8,128)(2,1)}), bf16[1,128,8,384]{3,2,0,1:T(8,128)(2,1)S(1)}, u32[]{:S(2)}, u32[]{:S(2)}) async-start(bf16[1,128,8,384]{3,2,0,1:T(8,128)(2,1)} %copy.156), calls=%async_computation.1 | async-start | bytes 1572864 | tf_op jit(solution)/shard_map/while/body/eval_jaxpr/all_to_all | solution.py:164
  (148 other events, 649.5 us)
Sparse Core Ops, SparseCore 0:
  10.2 71.5 all-gather.1
